TPU v7x, 256 devices: a whole 4x4x8 slice. The times are simulated.
256 devices in a mesh: mp: 64 (over z, x, core), head: 4 (over y).
Axes of the slice: x: 4, y: 4, z: 8, core: 2. Of those that a mesh axis runs over, the one named last changes fastest.
Arguments:
- hidden: bfloat16 [8, 4096], replicated, may hold values from -6 to 6
- norm_gain: float32 [4096], replicated, may hold values from 0.25 to 1.75
- w_query: bfloat16 [4096, 4096], P('mp', 'head'), may hold values from -0.09375 to 0.09375
- enc_states: bfloat16 [8, 4096, 4096], P(None, 'mp'), may hold values from -6 to 6
- w_key: bfloat16 [4096, 4096], P('mp', 'head'), may hold values from -0.09375 to 0.09375
- w_value: bfloat16 [4096, 4096], P('mp', 'head'), may hold values from -0.09375 to 0.09375
- w_out: bfloat16 [4096, 4096], P('head', 'mp'), may hold values from -0.09375 to 0.09375
- bias_table: float32 [32, 64], P(None, 'head'), may hold values from -5 to 300
- buckets: int32 [8, 4096], P(None, 'mp'), may hold values from 0 to 31
- src_len: int32 [8], replicated, may hold values from 512 to 4096
Outputs:
- updated: bfloat16 [8, 4096], P(None, 'mp')
All inputs are finite; a program needn't handle non-finite values.
Results may differ from a plain program's by a relative error of at most 0.0049.
Values may be sent and summed in bfloat16 or wider, within the bound.
A program may use at most 128 MiB of HBM per device.

v0:
```python
import jax
import jax.numpy as jnp
from jax import lax
from jax.sharding import PartitionSpec as P

EPSILON = 1e-06
NEGATIVE = -1e30


def shards(
    hidden, norm_gain, w_query, enc_states, w_key, w_value, w_out, bias_table, buckets, src_len
):
    batch, src_local, _ = enc_states.shape
    rows, inner = w_key.shape
    heads = bias_table.shape[1]
    head_size = inner // heads
    me = lax.axis_index("mp")
    widened = hidden.astype(jnp.float32)
    mean_square = jnp.mean(widened * widened, axis=-1, keepdims=True)
    normed = (widened * lax.rsqrt(mean_square + EPSILON) * norm_gain).astype(jnp.bfloat16)
    mine = lax.dynamic_slice_in_dim(normed, me * rows, rows, 1)
    query = jnp.dot(mine, w_query, preferred_element_type=jnp.float32)
    query = lax.psum(query, "mp").astype(jnp.bfloat16).reshape(batch, heads, head_size)
    probe = jnp.einsum(
        "bhe,dhe->bhd",
        query,
        w_key.reshape(rows, heads, head_size),
        preferred_element_type=jnp.float32,
    )
    probe = (probe * float(head_size) ** (-0.5)).astype(jnp.bfloat16)
    probe = lax.all_gather(probe, "mp", axis=2, tiled=True)
    scores = jnp.einsum("bhd,bsd->bhs", probe, enc_states, preferred_element_type=jnp.float32)
    ids = jnp.arange(bias_table.shape[0], dtype=jnp.int32)
    one_hot = (buckets[:, :, None] == ids[None, None, :]).astype(jnp.float32)
    scores = scores + jnp.einsum(
        "bsk,kh->bhs", one_hot, bias_table, precision=lax.Precision.HIGHEST
    )
    positions = me * src_local + jnp.arange(src_local, dtype=jnp.int32)
    live = (positions[None, :] < src_len[:, None])[:, None, :]
    scores = jnp.where(live, scores, NEGATIVE)
    top = lax.pmax(jnp.max(scores, axis=-1), "mp")
    weights = jnp.where(live, jnp.exp(scores - top[:, :, None]), 0.0)
    total = lax.psum(jnp.sum(weights, axis=-1), "mp")
    mixed = jnp.einsum(
        "bhs,bsd->bhd", weights.astype(jnp.bfloat16), enc_states, preferred_element_type=jnp.float32
    )
    mixed = lax.psum_scatter(mixed, "mp", scatter_dimension=2, tiled=True)
    mixed = (mixed / total[:, :, None]).astype(jnp.bfloat16)
    context = jnp.einsum(
        "bhd,dhe->bhe",
        mixed,
        w_value.reshape(rows, heads, head_size),
        preferred_element_type=jnp.float32,
    )
    context = lax.psum(context, "mp").astype(jnp.bfloat16).reshape(batch, inner)
    out = lax.psum(jnp.dot(context, w_out, preferred_element_type=jnp.float32), "head")
    cols = w_out.shape[1]
    residual = lax.dynamic_slice_in_dim(widened, me * cols, cols, 1)
    return (out + residual).astype(jnp.bfloat16)


def solution(mesh):
    in_specs = (
        P(),
        P(),
        P("mp", "head"),
        P(None, "mp", None),
        P("mp", "head"),
        P("mp", "head"),
        P("head", "mp"),
        P(None, "head"),
        P(None, "mp"),
        P(),
    )
    return jax.shard_map(
        shards, mesh=mesh, in_specs=in_specs, out_specs=P(None, "mp"), check_vma=False
    )
```

profile of v0, /device:TPU:0, one launch (start us, length us, event | category | flops | bytes accessed | tf_op | source)
XLA Modules:
  0.0 922.8 jit_solution(14839864621208806205)
XLA Ops:
  6.5 0.9 convert_element_type.28
  7.4 1.0 multiply_reduce_fusion
  8.4 0.8 dynamic-slice
  9.2 0.2 fusion.19
  9.4 251.9 %psum.28 = bf16[8,1024]{1,0:T(8,128)(2,1)S(1)} all-reduce(f32[8,1024]{1,0:T(8,128)S(1)} %fusion.19), channel_id=1, replica_groups=mesh['mp'=64,'head'=4] {'mp'}, use_global_device_ids=true, to_apply=%region_1.0 | all-reduce | flops 8192 | bytes 49152 | tf_op jit(solution)/shard_map/psum | solution.py:23
  261.4 1.1 reshape.52
  262.5 0.3 fusion.5
  262.7 0.8 copy.16
  263.6 0.7 broadcast_compare_fusion
  264.4 77.1 %all-gather.2.cloned.1.call-done = bf16[8,16,4096]{1,0,2:T(8,128)(2,1)} async-done(((bf16[8,16,64]{1,0,2:T(8,128)(2,1)}), bf16[8,16,4096]{1,0,2:T(8,128)(2,1)}) %all-gather.2.cloned.1.call-update) | async-done | bytes 1048592 | tf_op jit(solution)/shard_map/all_gather | solution.py:31
  341.5 7.3 fusion
  348.8 0.3 fusion.24
  349.1 126.0 %pmax.7 = f32[8,16]{1,0:T(8,128)S(1)} all-reduce(f32[8,16]{1,0:T(8,128)S(1)} %get-tuple-element.5), channel_id=1, replica_groups=mesh['mp'=64,'head'=4] {'mp'}, use_global_device_ids=true, to_apply=%region_3.4 | all-reduce | flops 128 | bytes 1024 | tf_op jit(solution)/shard_map/pmax | solution.py:41
  475.1 2.9 fusion.11
  478.0 16.8 %copy.22 = f32[8,16,4096]{0,1,2:T(8,128)} copy(f32[8,16,4096]{2,1,0:T(8,128)S(1)} %fusion.11) | data formatting | bytes 4194304
  494.8 23.7 %reshape.56 = f32[4096,128]{1,0:T(8,128)} reshape(f32[4096,16,8]{2,1,0:T(8,128)} %bitcast.23) | data formatting | bytes 4194304
  518.9 124.3 %psum.29 = f32[8,16]{1,0:T(8,128)S(1)} all-reduce(f32[8,16]{1,0:T(8,128)S(1)} %fusion.9), channel_id=1, replica_groups=mesh['mp'=64,'head'=4] {'mp'}, use_global_device_ids=true, to_apply=%region_6.7 | all-reduce | flops 128 | bytes 1024 | tf_op jit(solution)/shard_map/psum | solution.py:43
  643.3 13.6 %reduce-scatter.4.cloned.1.call-done = f32[64,128]{1,0:T(8,128)} async-done(((f32[4096,128]{1,0:T(8,128)}), f32[64,128]{1,0:T(8,128)}) %reduce-scatter.4.cloned.1.call-update) | async-done | bytes 32784
  656.9 1.0 reshape.57
  658.0 0.2 copy.23
  658.2 0.2 convolution_bitcast_fusion
  658.5 246.1 %psum.30 = bf16[8,16,64]{2,0,1:T(8,128)(2,1)S(1)} all-reduce(f32[8,16,64]{2,0,1:T(8,128)S(1)} %convolution_bitcast_fusion), channel_id=1, replica_groups=mesh['mp'=64,'head'=4] {'mp'}, use_global_device_ids=true, to_apply=%region_7.8 | all-reduce | flops 8192 | bytes 49152 | tf_op jit(solution)/shard_map/psum | solution.py:55
  904.9 10.5 %psum.31 = f32[8,64]{1,0:T(8,128)S(1)} all-reduce(f32[8,64]{1,0:T(8,128)S(1)} %fusion.25), channel_id=1, replica_groups=mesh['mp'=64,'head'=4] {'head'}, use_global_device_ids=true, to_apply=%region_8.9 | all-reduce | flops 512 | bytes 4096 | tf_op jit(solution)/shard_map/psum | solution.py:56
  915.3 0.7 add_convert_fusion
  (23 shorter events, 0.9 us)
Async XLA Ops:
  6.5 2.7 copy-start
  6.5 334.9 %all-gather.2.cloned.1.call-start = ((), (), s32[]{:S(2)}) async-start(), calls=%async_computation.1 | async-start | bytes 8519680 | tf_op jit(solution)/shard_map/all_gather | solution.py:31
  263.6 393.4 %reduce-scatter.4.cloned.1.call-start = ((), (), s32[]{:S(2)}) async-start(), calls=%async_computation.2 | async-start | bytes 2129920
  264.4 84.4 %copy-start.3 = (f32[32,16]{0,1:T(8,128)S(1)}, f32[32,16]{0,1:T(8,128)}, u32[]{:S(2)}) copy-start(f32[32,16]{0,1:T(8,128)} %param.17) | copy-start | bytes 6148
  264.4 84.4 %copy-start.4 = (s32[8,64]{1,0:T(8,128)S(1)}, s32[8,64]{1,0:T(8,128)}, u32[]{:S(2)}) copy-start(s32[8,64]{1,0:T(8,128)} %param.18) | copy-start | bytes 6148
  494.8 23.7 %copy-start.1 = (bf16[64,1024]{1,0:T(8,128)(2,1)S(1)}, bf16[64,1024]{1,0:T(8,128)(2,1)}, u32[]{:S(2)}) copy-start(bf16[64,1024]{1,0:T(8,128)(2,1)} %param.15) | copy-start | bytes 393220
  518.5 386.2 %copy-start.2 = (bf16[1024,64]{0,1:T(8,128)(2,1)S(1)}, bf16[1024,64]{0,1:T(8,128)(2,1)}, u32[]{:S(2)}) copy-start(bf16[1024,64]{0,1:T(8,128)(2,1)} %param.16) | copy-start | bytes 393220
Sparse Core Ops, SparseCore 0:
  263.7 77.7 all-gather.1
  518.7 138.2 reduce-scatter.3
where the time goes:
time: 924 us; the launch traced here: 923 us
  blocking collectives  759 us (82%)
  waiting for transfers between devices  90.8 us (10%)
  local copies, waits for them, and re-layouts  45 us (5%)
  between operations  13.5 us (1%)
  matrix products  11.3 us (1%)
    psum x1, blocking collectives, shards(): lax.psum(query, 'mp').astype(jnp.bfloat16).reshape(batch, heads, head_size)  252 us
    psum x1, blocking collectives, shards(): context = lax.psum(context, 'mp').astype(jnp.bfloat16).reshape(batch, inner)  246 us
    pmax x1, blocking collectives, shards(): top = lax.pmax(jnp.max(scores, axis=-1), 'mp')  126 us
    psum x1, blocking collectives, shards(): total = lax.psum(jnp.sum(weights, axis=-1), 'mp')  124 us
    all_gather x1, waiting for transfers between devices, shards(): probe = lax.all_gather(probe, 'mp', axis=2, tiled=True)  77.1 us
    unnamed x14, local copies, waits for them, and re-layouts  41.8 us
  transfers between devices with their start and end apart: 2, of which 2 were waited for; matrix products, arithmetic and copies ran while one was open for 0% of the time, Pallas kernels for 0%

commit v1 on v0

--- a/solution.py
+++ b/solution.py
@@ -5,6 +5,11 @@
 
 EPSILON = 1e-06
 NEGATIVE = -1e30
+
+
+def tiled_gather(array, axis, dim):
+    copies = jnp.concatenate([array] * lax.axis_size(axis), axis=dim)
+    return lax.all_to_all(copies, axis, dim, dim, tiled=True)
 
 
 def shards(
@@ -28,7 +33,7 @@
         preferred_element_type=jnp.float32,
     )
     probe = (probe * float(head_size) ** (-0.5)).astype(jnp.bfloat16)
-    probe = lax.all_gather(probe, "mp", axis=2, tiled=True)
+    probe = tiled_gather(probe, "mp", 2)
     scores = jnp.einsum("bhd,bsd->bhs", probe, enc_states, preferred_element_type=jnp.float32)
     ids = jnp.arange(bias_table.shape[0], dtype=jnp.int32)
     one_hot = (buckets[:, :, None] == ids[None, None, :]).astype(jnp.float32)

time: 924 us -> 907 us (0.982)
  waiting for transfers between devices: 90.8 us -> 42.9 us
  local copies, waits for them, and re-layouts: 45 us -> 73 us
    all_gather x1 -> x0, waiting for transfers between devices: 77.1 us -> none  [shards(): probe = lax.all_gather(probe, 'mp', axis=2, tiled=True)]
    all_to_all x0 -> x1, waiting for transfers between devices: none -> 28.7 us  [tiled_gather(): return lax.all_to_all(copies, axis, dim, dim, tiled=True)]
    unnamed x14 -> x18, local copies, waits for them, and re-layouts: 41.8 us -> 61.8 us
where the time goes in v1:
time: 907 us; the launch traced here: 906 us
  blocking collectives  758 us (84%)
  local copies, waits for them, and re-layouts  73 us (8%)
  waiting for transfers between devices  42.9 us (5%)
  between operations  13.5 us (1%)
  matrix products  11.3 us (1%)
    psum x1, blocking collectives, shards(): lax.psum(query, 'mp').astype(jnp.bfloat16).reshape(batch, heads, head_size)  252 us
    psum x1, blocking collectives, shards(): context = lax.psum(context, 'mp').astype(jnp.bfloat16).reshape(batch, inner)  246 us
    pmax x1, blocking collectives, shards(): top = lax.pmax(jnp.max(scores, axis=-1), 'mp')  125 us
    psum x1, blocking collectives, shards(): total = lax.psum(jnp.sum(weights, axis=-1), 'mp')  124 us
    unnamed x18, local copies, waits for them, and re-layouts  61.8 us
    all_to_all x1, waiting for transfers between devices, tiled_gather(): return lax.all_to_all(copies, axis, dim, dim, tiled=True)  28.7 us
  transfers between devices with their start and end apart: 2, of which 2 were waited for; matrix products, arithmetic and copies ran while one was open for 0% of the time, Pallas kernels for 0%

profile of v1, /device:TPU:0, one launch (start us, length us, event | category | flops | bytes accessed | tf_op | source)
XLA Modules:
  0.0 906.0 jit_solution(3862142294866757458)
XLA Ops:
  6.5 0.9 convert_element_type.28
  7.4 1.0 multiply_reduce_fusion
  8.4 0.8 dynamic-slice
  9.4 251.9 %psum.28 = bf16[8,1024]{1,0:T(8,128)(2,1)S(1)} all-reduce(f32[8,1024]{1,0:T(8,128)S(1)} %fusion.19), channel_id=1, replica_groups=mesh['mp'=64,'head'=4] {'mp'}, use_global_device_ids=true, to_apply=%region_1.0 | all-reduce | flops 8192 | bytes 49152 | tf_op jit(solution)/shard_map/psum | solution.py:28
  261.4 1.1 reshape.52
  262.5 0.2 fusion.5
  262.7 1.4 concatenate.3
  264.2 7.4 copy.16
  271.6 12.5 %reshape.58 = bf16[64,2,4096]{2,1,0:T(2,128)(2,1)} reshape(bf16[4096,8,16]{2,1,0:T(8,128)(2,1)} %bitcast.26) | data formatting | bytes 2097152
  284.0 4.7 all-to-all-start
  288.8 28.7 %all-to-all-done = bf16[64,2,4096]{2,1,0:T(2,128)(2,1)S(1)} async-done(((bf16[64,2,4096]{2,1,0:T(2,128)(2,1)}), bf16[64,2,4096]{2,1,0:T(2,128)(2,1)S(1)}, u32[]{:S(2)}, u32[]{:S(2)}) %all-to-all-start) | async-done | bytes 1048608 | tf_op jit(solution)/shard_map/all_to_all | solution.py:12
  317.6 7.5 reshape.59
  325.1 7.3 fusion
  332.4 0.3 fusion.24
  332.7 125.2 %pmax.7 = f32[8,16]{1,0:T(8,128)S(1)} all-reduce(f32[8,16]{1,0:T(8,128)S(1)} %get-tuple-element.5), channel_id=1, replica_groups=mesh['mp'=64,'head'=4] {'mp'}, use_global_device_ids=true, to_apply=%region_3.4 | all-reduce | flops 128 | bytes 1024 | tf_op jit(solution)/shard_map/pmax | solution.py:46
  457.9 2.9 fusion.11
  460.8 16.8 %copy.22 = f32[8,16,4096]{0,1,2:T(8,128)} copy(f32[8,16,4096]{2,1,0:T(8,128)S(1)} %fusion.11) | data formatting | bytes 4194304
  477.6 23.7 %reshape.56 = f32[4096,128]{1,0:T(8,128)} reshape(f32[4096,16,8]{2,1,0:T(8,128)} %bitcast.25) | data formatting | bytes 4194304
  501.7 124.2 %psum.29 = f32[8,16]{1,0:T(8,128)S(1)} all-reduce(f32[8,16]{1,0:T(8,128)S(1)} %fusion.9), channel_id=1, replica_groups=mesh['mp'=64,'head'=4] {'mp'}, use_global_device_ids=true, to_apply=%region_6.7 | all-reduce | flops 128 | bytes 1024 | tf_op jit(solution)/shard_map/psum | solution.py:48
  626.0 14.1 %reduce-scatter.4.cloned.1.call-done = f32[64,128]{1,0:T(8,128)} async-done(((f32[4096,128]{1,0:T(8,128)}), f32[64,128]{1,0:T(8,128)}) %reduce-scatter.4.cloned.1.call-update) | async-done | bytes 32784
  640.1 1.0 reshape.57
  641.6 246.1 %psum.30 = bf16[8,16,64]{2,0,1:T(8,128)(2,1)S(1)} all-reduce(f32[8,16,64]{2,0,1:T(8,128)S(1)} %convolution_bitcast_fusion), channel_id=1, replica_groups=mesh['mp'=64,'head'=4] {'mp'}, use_global_device_ids=true, to_apply=%region_7.8 | all-reduce | flops 8192 | bytes 49152 | tf_op jit(solution)/shard_map/psum | solution.py:60
  888.0 10.5 %psum.31 = f32[8,64]{1,0:T(8,128)S(1)} all-reduce(f32[8,64]{1,0:T(8,128)S(1)} %fusion.25), channel_id=1, replica_groups=mesh['mp'=64,'head'=4] {'head'}, use_global_device_ids=true, to_apply=%region_8.9 | all-reduce | flops 512 | bytes 4096 | tf_op jit(solution)/shard_map/psum | solution.py:61
  898.5 0.7 add_convert_fusion
  (27 shorter events, 1.6 us)
Async XLA Ops:
  6.5 2.7 copy-start
  271.6 17.2 %copy-start.5 = (s32[8]{0:T(128)S(1)}, s32[8]{0:T(128)}, u32[]{:S(2)}) copy-start(s32[8]{0:T(128)} %param.19) | copy-start | bytes 100
  284.0 33.5 %all-to-all-start = ((bf16[64,2,4096]{2,1,0:T(2,128)(2,1)}), bf16[64,2,4096]{2,1,0:T(2,128)(2,1)S(1)}, u32[]{:S(2)}, u32[]{:S(2)}) async-start(bf16[64,2,4096]{2,1,0:T(2,128)(2,1)} %reshape.58), calls=%async_computation | async-start | bytes 2097152 | tf_op jit(solution)/shard_map/all_to_all | solution.py:12
  288.7 351.4 %reduce-scatter.4.cloned.1.call-start = ((), (), s32[]{:S(2)}) async-start(), calls=%async_computation.2 | async-start | bytes 2129920
  325.1 7.3 copy-start.3
  325.1 7.3 copy-start.4
  477.6 23.7 %copy-start.1 = (bf16[64,1024]{1,0:T(8,128)(2,1)S(1)}, bf16[64,1024]{1,0:T(8,128)(2,1)}, u32[]{:S(2)}) copy-start(bf16[64,1024]{1,0:T(8,128)(2,1)} %param.15) | copy-start | bytes 393220
  501.3 386.6 %copy-start.2 = (bf16[1024,64]{0,1:T(8,128)(2,1)S(1)}, bf16[1024,64]{0,1:T(8,128)(2,1)}, u32[]{:S(2)}) copy-start(bf16[1024,64]{0,1:T(8,128)(2,1)} %param.16) | copy-start | bytes 393220
Sparse Core Ops, SparseCore 0:
  501.5 138.5 reduce-scatter.3

commit v2 on v0

--- a/solution.py
+++ b/solution.py
@@ -52,7 +52,9 @@
         w_value.reshape(rows, heads, head_size),
         preferred_element_type=jnp.float32,
     )
-    context = lax.psum(context, "mp").astype(jnp.bfloat16).reshape(batch, inner)
+    context = (
+        jnp.sum(lax.all_gather(context, "mp"), axis=0).astype(jnp.bfloat16).reshape(batch, inner)
+    )
     out = lax.psum(jnp.dot(context, w_out, preferred_element_type=jnp.float32), "head")
     cols = w_out.shape[1]
     residual = lax.dynamic_slice_in_dim(widened, me * cols, cols, 1)

time: 924 us -> 757 us (0.82)
  blocking collectives: 759 us -> 513 us
  waiting for transfers between devices: 90.8 us -> 166 us
    psum x1 -> x0, blocking collectives: 246 us -> none  [shards(): context = lax.psum(context, 'mp').astype(jnp.bfloat16).reshape(batch, inner)]
    all_gather x0 -> x1, waiting for transfers between devices: none -> 74.8 us  [shards(): lax.all_gather(context, 'mp')]
  transfers between devices with their start and end apart: 2 -> 3, of which waited for: 2 -> 3; matrix products, arithmetic and copies ran while one was open for 0% -> 0% of each run, Pallas kernels for 0% -> 0%
where the time goes in v2:
time: 757 us; the launch traced here: 754 us
  blocking collectives  513 us (68%)
  waiting for transfers between devices  166 us (22%)
  local copies, waits for them, and re-layouts  45 us (6%)
  between operations  13.2 us (2%)
  matrix products  12 us (2%)
    psum x1, blocking collectives, shards(): lax.psum(query, 'mp').astype(jnp.bfloat16).reshape(batch, heads, head_size)  252 us
    pmax x1, blocking collectives, shards(): top = lax.pmax(jnp.max(scores, axis=-1), 'mp')  126 us
    psum x1, blocking collectives, shards(): total = lax.psum(jnp.sum(weights, axis=-1), 'mp')  124 us
    all_gather x1, waiting for transfers between devices, shards(): probe = lax.all_gather(probe, 'mp', axis=2, tiled=True)  77.1 us
    all_gather x1, waiting for transfers between devices, shards(): lax.all_gather(context, 'mp')  74.8 us
    unnamed x14, local copies, waits for them, and re-layouts  41.8 us
  transfers between devices with their start and end apart: 3, of which 3 were waited for; matrix products, arithmetic and copies ran while one was open for 0% of the time, Pallas kernels for 0%

profile of v2, /device:TPU:0, one launch (start us, length us, event | category | flops | bytes accessed | tf_op | source)
XLA Modules:
  0.0 754.3 jit_solution(3215103407128692392)
XLA Ops:
  6.5 0.9 convert_element_type.32
  7.4 1.0 multiply_reduce_fusion
  8.4 0.8 dynamic-slice
  9.4 251.9 %psum.21 = bf16[8,1024]{1,0:T(8,128)(2,1)S(1)} all-reduce(f32[8,1024]{1,0:T(8,128)S(1)} %fusion.19), channel_id=1, replica_groups=mesh['mp'=64,'head'=4] {'mp'}, use_global_device_ids=true, to_apply=%region_1.0 | all-reduce | flops 8192 | bytes 49152 | tf_op jit(solution)/shard_map/psum | solution.py:23
  261.4 1.1 reshape.52
  262.5 0.3 fusion.5
  262.7 0.8 copy.17
  263.6 0.7 broadcast_compare_fusion
  264.4 77.1 %all-gather.4.cloned.1.call-done = bf16[8,16,4096]{1,0,2:T(8,128)(2,1)} async-done(((bf16[8,16,64]{1,0,2:T(8,128)(2,1)}), bf16[8,16,4096]{1,0,2:T(8,128)(2,1)}) %all-gather.4.cloned.1.call-update) | async-done | bytes 1048592 | tf_op jit(solution)/shard_map/all_gather | solution.py:31
  341.5 7.3 fusion
  348.8 0.3 fusion.24
  349.1 126.0 %pmax.7 = f32[8,16]{1,0:T(8,128)S(1)} all-reduce(f32[8,16]{1,0:T(8,128)S(1)} %get-tuple-element.5), channel_id=1, replica_groups=mesh['mp'=64,'head'=4] {'mp'}, use_global_device_ids=true, to_apply=%region_3.4 | all-reduce | flops 128 | bytes 1024 | tf_op jit(solution)/shard_map/pmax | solution.py:41
  475.1 2.9 fusion.11
  478.0 16.8 %copy.23 = f32[8,16,4096]{0,1,2:T(8,128)} copy(f32[8,16,4096]{2,1,0:T(8,128)S(1)} %fusion.11) | data formatting | bytes 4194304
  494.8 23.7 %reshape.56 = f32[4096,128]{1,0:T(8,128)} reshape(f32[4096,16,8]{2,1,0:T(8,128)} %bitcast.25) | data formatting | bytes 4194304
  519.0 124.3 %psum.22 = f32[8,16]{1,0:T(8,128)S(1)} all-reduce(f32[8,16]{1,0:T(8,128)S(1)} %fusion.9), channel_id=1, replica_groups=mesh['mp'=64,'head'=4] {'mp'}, use_global_device_ids=true, to_apply=%region_6.7 | all-reduce | flops 128 | bytes 1024 | tf_op jit(solution)/shard_map/psum | solution.py:43
  643.4 13.6 %reduce-scatter.4.cloned.1.call-done = f32[64,128]{1,0:T(8,128)} async-done(((f32[4096,128]{1,0:T(8,128)}), f32[64,128]{1,0:T(8,128)}) %reduce-scatter.4.cloned.1.call-update) | async-done | bytes 32784
  657.0 1.0 reshape.57
  658.0 0.3 copy.24
  658.3 0.9 convolution_bitcast_fusion
  659.2 74.8 %all-gather.6.cloned.1.call-done = f32[512,16,64]{2,0,1:T(8,128)} async-done(((f32[8,16,64]{2,0,1:T(8,128)}), f32[512,16,64]{2,0,1:T(8,128)}) %all-gather.6.cloned.1.call-update) | async-done | bytes 2097168 | tf_op jit(solution)/shard_map/all_gather | solution.py:56
  734.0 2.5 bitcast_reduce_fusion
  736.7 10.5 %psum.23 = f32[8,64]{1,0:T(8,128)S(1)} all-reduce(f32[8,64]{1,0:T(8,128)S(1)} %fusion.25), channel_id=1, replica_groups=mesh['mp'=64,'head'=4] {'head'}, use_global_device_ids=true, to_apply=%region_8.9 | all-reduce | flops 512 | bytes 4096 | tf_op jit(solution)/shard_map/psum | solution.py:58
  747.2 0.7 add_convert_fusion
  (26 shorter events, 1.1 us)
Async XLA Ops:
  6.5 2.7 copy-start
  6.5 334.9 %all-gather.4.cloned.1.call-start = ((), (), s32[]{:S(2)}) async-start(), calls=%async_computation.1 | async-start | bytes 8519680 | tf_op jit(solution)/shard_map/all_gather | solution.py:31
  263.6 393.4 %reduce-scatter.4.cloned.1.call-start = ((), (), s32[]{:S(2)}) async-start(), calls=%async_computation.3 | async-start | bytes 2129920
  264.4 84.4 %copy-start.3 = (f32[32,16]{0,1:T(8,128)S(1)}, f32[32,16]{0,1:T(8,128)}, u32[]{:S(2)}) copy-start(f32[32,16]{0,1:T(8,128)} %param.17) | copy-start | bytes 6148
  264.4 84.4 %copy-start.4 = (s32[8,64]{1,0:T(8,128)S(1)}, s32[8,64]{1,0:T(8,128)}, u32[]{:S(2)}) copy-start(s32[8,64]{1,0:T(8,128)} %param.18) | copy-start | bytes 6148
  494.8 23.8 %copy-start.1 = (bf16[64,1024]{1,0:T(8,128)(2,1)S(1)}, bf16[64,1024]{1,0:T(8,128)(2,1)}, u32[]{:S(2)}) copy-start(bf16[64,1024]{1,0:T(8,128)(2,1)} %param.15) | copy-start | bytes 393220
  518.5 218.0 %copy-start.2 = (bf16[1024,64]{0,1:T(8,128)(2,1)S(1)}, bf16[1024,64]{0,1:T(8,128)(2,1)}, u32[]{:S(2)}) copy-start(bf16[1024,64]{0,1:T(8,128)(2,1)} %param.16) | copy-start | bytes 393220
  518.5 215.4 %all-gather.6.cloned.1.call-start = ((), (), s32[]{:S(2)}) async-start(), calls=%async_computation.2 | async-start | bytes 4259840 | tf_op jit(solution)/shard_map/all_gather | solution.py:56
Sparse Core Ops, SparseCore 0:
  263.7 77.7 all-gather.3
  518.7 138.2 reduce-scatter.3
  659.6 74.3 all-gather.5
